TPU v7x, 128 devices: a whole 4x4x4 slice. The times are simulated.
128 devices in a mesh: grp: 4 (over z), wave: 32 (over x, y, core).
Axes of the slice: x: 4, y: 4, z: 4, core: 2. Of those that a mesh axis runs over, the one named last changes fastest.
Arguments:
- state: bfloat16 [275, 984320], P(None, ('grp', 'wave')), may hold values from -6 to 6
- held_orders: int32 [640], P(('grp', 'wave')), may hold values from -1 to 383, as said below
- pair_lows: int32 [384], P(('grp', 'wave')), may hold values from 0 to 383, each once
- inverses: bfloat16 [384, 2, 137, 137], P(('grp', 'wave')), may hold values from -2 to 3
- height_operator: bfloat16 [137, 137], replicated, may hold values from -0.5 to 0.5
- pressure_column: bfloat16 [137], replicated, may hold values from -5 to 5
- thermal_response_matrix: bfloat16 [137, 137], replicated, may hold values from -0.5 to 0.5
- mass_row: bfloat16 [137], replicated, may hold values from -0.5 to 0.5
Outputs:
- advanced: bfloat16 [275, 984320], P(None, ('grp', 'wave'))
Inputs may be any that keep to these rules, and one draw needn't show every extreme that they name: `held_orders`: each of 0 to 383 appears exactly once, all other entries are -1; some device has all 5 of its slots filled.
All inputs are finite; a program needn't handle non-finite values.
Results may differ from a plain program's by a relative error of at most 0.0052.
Values may be sent and summed in bfloat16 or wider, within the bound.
A program may use at most 128 MiB of HBM per device.

v0:
```python
import jax
import jax.numpy as jnp
from jax import lax
from jax.sharding import Mesh
from jax.sharding import PartitionSpec as P

GRP_WAVE = ("grp", "wave_0", "wave_1", "wave_2")
WAVE = ("wave_0", "wave_1", "wave_2")


def in_order(tiles, dim):
    shape = list(tiles.shape[1:])
    shape[dim] *= tiles.shape[0]
    return jnp.moveaxis(tiles, 0, dim).reshape(shape)


def all_blocks(shard, axes, turns):
    tiles = shard[None]
    for k in turns:
        tiles = lax.all_gather(tiles, axes[k], axis=0, tiled=True)
    held = [lax.axis_size(axes[k]) for k in reversed(turns)]
    tiles = tiles.reshape(*held, *shard.shape)
    turned = sorted(range(len(turns)), key=lambda place: turns[len(turns) - 1 - place])
    return tiles.transpose(*turned, *range(len(turns), tiles.ndim)).reshape(-1, *shard.shape)


def gathered_by_axis(shard, axes, turns, dim):
    return in_order(all_blocks(shard, axes, turns), dim)


def send_out(message):
    return lax.all_to_all(message, GRP_WAVE, split_axis=1, concat_axis=1, tiled=True)


def send_home(message):
    return lax.all_to_all(message, GRP_WAVE, split_axis=1, concat_axis=1, tiled=True)


def solve_columns(inverses, right_side, low_mask, split):
    upper = jnp.einsum(
        "jkl,lajc->kajc", inverses[:, 1], right_side, preferred_element_type=jnp.float32
    )
    lower = jnp.einsum(
        "jkl,lajc->kajc",
        inverses[:, 0],
        right_side[..., :split],
        preferred_element_type=jnp.float32,
    )
    first = jnp.where(low_mask[None, :, :, :split], lower, upper[..., :split])
    return jnp.concatenate([first, upper[..., split:]], axis=-1).astype(jnp.bfloat16)


def shards(
    state,
    held_orders,
    pair_lows,
    inverses,
    height_operator,
    pressure_column,
    thermal_response_matrix,
    mass_row,
):
    layer_heights_count = height_operator.shape[0]
    pair_count = pair_lows.shape[0]
    slot_count = held_orders.shape[0]
    devices = lax.axis_size("grp") * lax.axis_size(WAVE)
    truncation = 2 * pair_count * devices - 1
    slot_width = 2 * (truncation + 2)
    denom = float(truncation * (truncation + 1))
    fill_col = slot_count * slot_width
    all_lows = gathered_by_axis(pair_lows, (("grp", "wave_0", "wave_1"), "wave_2"), (0, 1), 0)
    own_low = pair_lows.reshape(1, pair_count, 1)
    all_orders = gathered_by_axis(held_orders, GRP_WAVE, (0, 1, 2, 3), 0)
    low_grid = all_lows.reshape(devices, pair_count, 1, 1)
    orders = held_orders.reshape(1, 1, slot_count, 1)
    halves = jnp.arange(2, dtype=jnp.int32).reshape(1, 1, 1, 2)
    slot_ids = jnp.arange(slot_count, dtype=jnp.int32).reshape(1, 1, slot_count, 1)
    live = orders >= 0

    def place(position):
        spot = slot_ids * slot_width + 2 * position + halves
        return jnp.where(live, spot, fill_col).reshape(devices, pair_count, -1)

    first = place(jnp.where(orders <= low_grid, low_grid - orders, truncation + 1 - low_grid))
    second = place(truncation - low_grid - orders)
    hit = orders == low_grid
    found = jnp.any(hit, axis=2)
    slot_hit = jnp.sum(jnp.where(hit, slot_ids, 0), axis=2)
    extra = slot_hit * slot_width + 2 * (truncation + 1 - low_grid[:, :, 0]) + halves[:, :, 0]
    extra = jnp.where(found, extra, fill_col)
    column = jnp.concatenate([first, second, extra], axis=2).reshape(-1)
    source_orders = all_orders.reshape(devices, 1, slot_count, 1)
    low_first = jnp.broadcast_to(
        source_orders <= own_low[..., None], (devices, pair_count, slot_count, 2)
    ).reshape(devices, pair_count, -1)
    low_mask = jnp.concatenate(
        [low_first, jnp.zeros((devices, pair_count, 2 * slot_count + 2), jnp.bool_)], axis=2
    )
    split = 2 * slot_count
    per_pair = low_mask.shape[2]
    recv_shape = (devices, pair_count, per_pair)
    divergence = state[:layer_heights_count]
    thermal_state_array = state[layer_heights_count : 2 * layer_heights_count]
    pressure = state[2 * layer_heights_count]
    coeff_index = (jnp.arange(slot_width, dtype=jnp.int32) // 2)[None, :]
    order_col = held_orders[:, None]
    degree = jnp.where(
        coeff_index <= truncation - order_col, order_col + coeff_index, coeff_index - 1
    )
    lap_scale = ((degree * (degree + 1)).astype(jnp.float32) / denom).reshape(-1)
    height_drive_term = jnp.dot(
        height_operator, thermal_state_array, preferred_element_type=jnp.float32
    )
    height_drive_term = (
        height_drive_term
        + pressure_column.astype(jnp.float32)[:, None] * pressure.astype(jnp.float32)[None, :]
    )
    right_side = (divergence.astype(jnp.float32) + lap_scale[None, :] * height_drive_term).astype(
        jnp.bfloat16
    )
    message = jnp.take(right_side, column, axis=1, mode="fill", fill_value=0)
    arriving_arrays = send_out(message).reshape((layer_heights_count,) + recv_shape)
    div_sent = solve_columns(inverses, arriving_arrays, low_mask, split).reshape(
        layer_heights_count, -1
    )
    returned = send_home(div_sent)
    next_spreading_rate = (
        jnp.zeros((layer_heights_count, fill_col), jnp.bfloat16)
        .at[:, column]
        .set(returned, mode="drop")
    )
    next_thermal_state = (
        thermal_state_array.astype(jnp.float32)
        - jnp.dot(thermal_response_matrix, next_spreading_rate, preferred_element_type=jnp.float32)
    ).astype(jnp.bfloat16)
    surface_mass_next = (
        pressure.astype(jnp.float32)
        - jnp.dot(mass_row, next_spreading_rate, preferred_element_type=jnp.float32)
    ).astype(jnp.bfloat16)
    live_slot = jnp.repeat(held_orders >= 0, slot_width)[None, :]
    result = jnp.concatenate(
        [next_spreading_rate, next_thermal_state, surface_mass_next[None, :]], axis=0
    )
    return jnp.where(live_slot, result, jnp.zeros_like(result))


def solution(mesh):
    torus = Mesh(
        mesh.devices.reshape(mesh.shape["grp"], 4, 4, 2), ("grp", "wave_0", "wave_1", "wave_2")
    )
    placed = (
        P(None, GRP_WAVE),
        P(GRP_WAVE),
        P(GRP_WAVE),
        P(GRP_WAVE, None, None, None),
        P(),
        P(),
        P(),
        P(),
    )
    return jax.shard_map(
        shards, mesh=torus, in_specs=placed, out_specs=P(None, GRP_WAVE), check_vma=False
    )
```

profile of v0, /device:TPU:1, one launch (start us, length us, event | category | flops | bytes accessed | tf_op | source)
XLA Modules:
  0.0 343.3 jit_solution(1832600771421519429)
XLA Ops:
  0.0 1.3 dynamic-slice
  1.9 0.9 dynamic-update-slice
  2.8 20.8 %all-reduce = s32[192]{0:T(256)S(1)} all-reduce(s32[192]{0:T(256)S(1)} %dynamic-update-slice), channel_id=2, replica_groups=mesh['grp'=4,'wave_0'=4,'wave_1'=4,'wave_2'=2] {'grp','wave_0','wave_1'}, use_global_device_ids=true, to_apply=%add | all-reduce | flops 192 | bytes 1536
  23.6 0.1 reshape.256
  23.8 7.4 %all-gather.2 = s32[2,64,3]{1,2,0:T(4,128)S(1)} all-gather(s32[1,64,3]{1,2,0:T(4,128)S(1)} %copy.56), channel_id=1, replica_groups=mesh['grp'=4,'wave_0'=4,'wave_1'=4,'wave_2'=2] {'wave_2'}, dimensions={0}, use_global_device_ids=true | all-gather | bytes 2304 | tf_op jit(solution)/shard_map/all_gather | solution.py:20
  31.2 0.1 copy.57
  31.3 0.1 le.77
  31.4 0.7 broadcast_compare_fusion.1
  32.1 0.7 fusion.15
  32.8 0.7 compare_reduce_fusion
  33.6 0.7 broadcast_subtract_fusion.2
  34.3 0.7 multiply_add_fusion.1
  35.1 0.1 broadcast_in_dim.123
  35.2 0.1 add.162
  35.4 0.2 copy.59
  35.6 0.2 reshape.227
  35.8 0.1 fusion.9
  36.0 0.7 add_select_fusion
  36.7 0.1 select_n.101
  36.8 1.0 convert_reduce_fusion
  37.8 0.7 convert_element_type.37
  38.5 3.9 %fusion.4 = bf16[137,7690]{1,0:T(8,128)(2,1)S(1)} fusion(bf16[137,137]{1,0:T(8,128)(2,1)S(1)} %copy-done, f32[7690]{0:T(1024)S(1)} %convert_reduce_fusion, f32[137]{0:T(256)S(1)} %convert_element_type.37, f32[7690]{0:T(1024)S(1)} %fusion.11, bf16[275,7690]{1,0:T(8,128)(2,1)} %param.8), kind=kOutput, calls=%fused_computation.8 | convolution fusion | flops 294988448 | bytes 6704074 | tf_op jit(solution)/shard_map/dot_general | solution.py:111
  42.4 3.7 %copy.67 = bf16[137,7690]{0,1:T(8,128)(2,1)} copy(bf16[137,7690]{1,0:T(8,128)(2,1)S(1)} %fusion.4) | data formatting | bytes 4214120 | tf_op jit(solution)/shard_map/convert_element_type | solution.py:118
  46.1 22.6 %gather_fusion = bf16[8448,137]{1,0:T(8,128)(2,1)} fusion(bf16[137,7690]{0,1:T(8,128)(2,1)} %copy.67, s32[9216]{0:T(1024)S(1)} %pad_clamp_fusion), kind=kCustom, calls=%fused_computation | custom fusion | bytes 4663296 | tf_op jit(solution)/shard_map/jit(_take)/gather | solution.py:121
  68.8 5.0 %copy.68 = bf16[137,8448]{1,0:T(8,128)(2,1)S(1)} copy(bf16[137,8448]{0,1:T(8,128)(2,1)} %bitcast.62) | data formatting | bytes 4629504 | tf_op jit(solution)/shard_map/jit(_take)/gather | solution.py:121
  73.8 16.8 %gather.7 = bf16[137,128,66]{2,1,0:T(8,128)(2,1)} reshape(bf16[137,8448]{1,0:T(8,128)(2,1)S(1)} %copy.68) | data formatting | bytes 4629504 | tf_op jit(solution)/shard_map/jit(_take)/gather | solution.py:121
  90.5 0.1 copy.66
  90.7 2.6 broadcast_select_fusion
  93.2 5.0 %copy.88 = bf16[137,128,66]{2,0,1:T(8,128)(2,1)} copy(bf16[137,128,66]{2,1,0:T(8,128)(2,1)S(1)} %broadcast_select_fusion) | data formatting | bytes 4629504 | tf_op jit(solution)/shard_map/jit(_take)/select_n | solution.py:121
  98.3 17.0 %reshape.283 = bf16[128,2,4521]{2,1,0:T(2,128)(2,1)} reshape(bf16[128,137,66]{2,1,0:T(8,128)(2,1)} %bitcast.58) | data formatting | bytes 4629504
  115.3 3.9 %all-to-all-start = ((bf16[128,2,4521]{2,1,0:T(2,128)(2,1)}), bf16[128,2,4521]{2,1,0:T(2,128)(2,1)S(1)}, u32[]{:S(2)}, u32[]{:S(2)}) async-start(bf16[128,2,4521]{2,1,0:T(2,128)(2,1)} %reshape.283), calls=%async_computation | async-start | bytes 4718592 | tf_op jit(solution)/shard_map/all_to_all | solution.py:32
  119.3 0.7 dynamic-slice.1
  120.6 0.2 dynamic-update-slice.1
  120.9 13.8 %all-reduce.1 = s32[20]{0:T(128)S(1)} all-reduce(s32[20]{0:T(128)S(1)} %dynamic-update-slice.1), channel_id=3, replica_groups=mesh['grp'=4,'wave_0'=4,'wave_1'=4,'wave_2'=2] {'grp'}, use_global_device_ids=true, to_apply=%add.1 | all-reduce | flops 20 | bytes 160
  134.7 0.1 reshape.258
  134.8 15.7 %all-gather.3 = s32[4,4,5]{2,1,0:T(4,128)S(1)} all-gather(s32[1,4,5]{2,1,0:T(4,128)S(1)} %reshape.258), channel_id=1, replica_groups=mesh['grp'=4,'wave_0'=4,'wave_1'=4,'wave_2'=2] {'wave_0'}, dimensions={0}, use_global_device_ids=true | all-gather | bytes 400 | tf_op jit(solution)/shard_map/all_gather | solution.py:20
  150.5 0.1 copy.79
  150.5 16.4 %all-gather.4 = s32[4,16,5]{1,2,0:T(8,128)S(1)} all-gather(s32[1,16,5]{1,2,0:T(8,128)S(1)} %copy.79), channel_id=1, replica_groups=mesh['grp'=4,'wave_0'=4,'wave_1'=4,'wave_2'=2] {'wave_1'}, dimensions={0}, use_global_device_ids=true | all-gather | bytes 1600 | tf_op jit(solution)/shard_map/all_gather | solution.py:20
  167.0 0.1 reshape.262
  167.0 10.1 %all-gather.5 = s32[2,64,5]{1,2,0:T(8,128)S(1)} all-gather(s32[1,64,5]{1,2,0:T(8,128)S(1)} %reshape.262), channel_id=1, replica_groups=mesh['grp'=4,'wave_0'=4,'wave_1'=4,'wave_2'=2] {'wave_2'}, dimensions={0}, use_global_device_ids=true | all-gather | bytes 3840 | tf_op jit(solution)/shard_map/all_gather | solution.py:20
  177.2 0.1 reshape.228
  177.3 0.3 copy.63
  177.9 1.3 fusion.16
  179.2 10.2 %reshape.284 = bf16[128,137,66]{2,1,0:T(8,128)(2,1)} reshape(bf16[128,2,4521]{2,1,0:T(2,128)(2,1)S(1)} %all-to-all-done) | data formatting | bytes 4629504
  189.4 6.0 %copy.70 = bf16[137,128,66]{1,0,2:T(8,128)(2,1)S(1)} copy(bf16[137,128,66]{2,0,1:T(8,128)(2,1)} %bitcast.59) | data formatting | bytes 4629504 | tf_op jit(solution)/shard_map/all_to_all | solution.py:32
  195.4 0.8 convolution_bitcast_fusion.1
  196.3 0.1 slice.46
  196.3 0.1 copy-done.4
  196.4 0.4 fusion.5
  196.9 0.2 pad_maximum_fusion
  197.1 4.9 %copy.73 = bf16[137,128,66]{2,0,1:T(8,128)(2,1)} copy(bf16[137,128,66]{1,0,2:T(8,128)(2,1)S(1)} %bitcast.66) | data formatting | bytes 4629504 | tf_op jit(solution)/shard_map/convert_element_type | solution.py:50
  202.1 16.8 %reshape.285 = bf16[128,2,4521]{2,1,0:T(2,128)(2,1)} reshape(bf16[128,137,66]{2,1,0:T(8,128)(2,1)} %bitcast.60) | data formatting | bytes 4629504
  218.9 5.6 %all-to-all-start.1 = ((bf16[128,2,4521]{2,1,0:T(2,128)(2,1)}), bf16[128,2,4521]{2,1,0:T(2,128)(2,1)S(1)}, u32[]{:S(2)}, u32[]{:S(2)}) async-start(bf16[128,2,4521]{2,1,0:T(2,128)(2,1)} %reshape.285), calls=%async_computation.1 | async-start | bytes 4718592 | tf_op jit(solution)/shard_map/all_to_all | solution.py:36
  224.7 0.1 broadcast_in_dim.119
  224.8 32.9 %all-to-all-done.1 = bf16[128,2,4521]{2,1,0:T(2,128)(2,1)S(1)} async-done(((bf16[128,2,4521]{2,1,0:T(2,128)(2,1)}), bf16[128,2,4521]{2,1,0:T(2,128)(2,1)S(1)}, u32[]{:S(2)}, u32[]{:S(2)}) %all-to-all-start.1) | async-done | bytes 2314784 | tf_op jit(solution)/shard_map/all_to_all | solution.py:36
  257.7 10.2 %reshape.286 = bf16[128,137,66]{2,1,0:T(8,128)(2,1)} reshape(bf16[128,2,4521]{2,1,0:T(2,128)(2,1)S(1)} %all-to-all-done.1) | data formatting | bytes 4629504
  267.9 5.6 %copy.74 = bf16[137,128,66]{2,1,0:T(8,128)(2,1)} copy(bf16[137,128,66]{2,0,1:T(8,128)(2,1)} %bitcast.61) | data formatting | bytes 4629504 | tf_op jit(solution)/shard_map/all_to_all | solution.py:36
  273.5 7.4 %reshape.241 = bf16[137,8448]{1,0:T(8,128)(2,1)S(1)} reshape(bf16[137,128,66]{2,1,0:T(8,128)(2,1)} %copy.74) | data formatting | bytes 4629504 | tf_op jit(solution)/shard_map/all_to_all | solution.py:36
  280.9 3.8 %copy.75 = bf16[8448,137]{1,0:T(8,128)(2,1)} copy(bf16[8448,137]{0,1:T(8,128)(2,1)S(1)} %bitcast.65) | data formatting | bytes 4629504 | tf_op jit(solution)/shard_map/all_to_all | solution.py:36
  284.7 44.6 %scatter_custom_fusion = bf16[137,7690]{0,1:T(8,128)(2,1)} fusion(s32[8448]{0:T(1024)S(1)} %fusion.9, bf16[8448,137]{1,0:T(8,128)(2,1)} %copy.75, bf16[]{:T(256)} %constant.21.clone.1), kind=kCustom, calls=%fused_computation.17 | custom fusion | bytes 2107572 | tf_op jit(solution)/shard_map/scatter | solution.py:130
  329.3 4.6 %copy.76 = bf16[137,7690]{1,0:T(8,128)(2,1)S(1)} copy(bf16[137,7690]{0,1:T(8,128)(2,1)} %scatter_custom_fusion) | data formatting | bytes 4214120 | tf_op jit(solution)/shard_map/scatter | solution.py:130
  334.0 4.5 %fusion.3 = bf16[137,7690]{1,0:T(8,128)(2,1)S(1)} fusion(bf16[137,7690]{0,1:T(8,128)(2,1)} %scatter_custom_fusion, bf16[137,137]{1,0:T(8,128)(2,1)S(1)} %copy-done.7, bf16[275,7690]{1,0:T(8,128)(2,1)} %param.8), kind=kOutput, calls=%fused_computation.7 | convolution fusion | flops 291827840 | bytes 6358718 | tf_op jit(solution)/shard_map/dot_general | solution.py:134
  338.5 1.1 convolution_reduce_fusion
  339.7 3.3 maximum_select_fusion
  (49 shorter events, 0.7 us)
Async XLA Ops:
  0.0 38.5 %copy-start = (bf16[137,137]{1,0:T(8,128)(2,1)S(1)}, bf16[137,137]{1,0:T(8,128)(2,1)}, u32[]{:S(2)}) copy-start(bf16[137,137]{1,0:T(8,128)(2,1)} %param.12) | copy-start | bytes 112618
  115.3 4.0 %copy-start.9 = (u32[128]{0:T(128)S(1)}, u32[128]{0:T(128)}, u32[]{:S(2)}) copy-start(u32[128]{0:T(128)} %constant.72) | copy-start | bytes 1540
  115.3 5.3 %copy-start.5 = (s32[5]{0:T(128)S(1)}, s32[5]{0:T(128)}, u32[]{:S(2)}) copy-start(s32[5]{0:T(128)} %param.9) | copy-start | bytes 64
  115.3 62.4 %copy-start.6 = (s32[3]{0:T(128)S(1)}, s32[3]{0:T(128)}, u32[]{:S(2)}) copy-start(s32[3]{0:T(128)} %param.10) | copy-start | bytes 40
  115.3 62.6 %copy-start.3 = (bf16[3,2,137,137]{3,1,2,0:T(2,128)(2,1)S(1)}, bf16[3,2,137,137]{3,1,2,0:T(2,128)(2,1)}, u32[]{:S(2)}) copy-start(bf16[3,2,137,137]{3,1,2,0:T(2,128)(2,1)} %param.11) | copy-start | bytes 675688
  115.3 63.9 %all-to-all-start = ((bf16[128,2,4521]{2,1,0:T(2,128)(2,1)}), bf16[128,2,4521]{2,1,0:T(2,128)(2,1)S(1)}, u32[]{:S(2)}, u32[]{:S(2)}) async-start(bf16[128,2,4521]{2,1,0:T(2,128)(2,1)} %reshape.283), calls=%async_computation | async-start | bytes 4718592 | tf_op jit(solution)/shard_map/all_to_all | solution.py:32
  195.4 1.0 copy-start.4
  218.9 5.7 %copy-start.8 = (bf16[137]{0:T(256)(128)(2,1)S(1)}, bf16[137]{0:T(256)(128)(2,1)}, u32[]{:S(2)}) copy-start(bf16[137]{0:T(256)(128)(2,1)} %param.15) | copy-start | bytes 826
  218.9 38.8 %all-to-all-start.1 = ((bf16[128,2,4521]{2,1,0:T(2,128)(2,1)}), bf16[128,2,4521]{2,1,0:T(2,128)(2,1)S(1)}, u32[]{:S(2)}, u32[]{:S(2)}) async-start(bf16[128,2,4521]{2,1,0:T(2,128)(2,1)} %reshape.285), calls=%async_computation.1 | async-start | bytes 4718592 | tf_op jit(solution)/shard_map/all_to_all | solution.py:36
  329.3 4.6 %copy-start.7 = (bf16[137,137]{1,0:T(8,128)(2,1)S(1)}, bf16[137,137]{1,0:T(8,128)(2,1)}, u32[]{:S(2)}) copy-start(bf16[137,137]{1,0:T(8,128)(2,1)} %param.14) | copy-start | bytes 112618
  334.0 4.5 %copy-start.2 = (bf16[137,7690]{0,1:T(8,128)(2,1)S(1)}, bf16[137,7690]{0,1:T(8,128)(2,1)}, u32[]{:S(2)}) copy-start(bf16[137,7690]{0,1:T(8,128)(2,1)} %scatter_custom_fusion) | copy-start | bytes 6321184
  339.7 3.4 copy-start.1
where the time goes:
time: 348 us; the launch traced here: 343 us
  local copies, waits for them, and re-layouts  191 us (55%)
  blocking collectives  84.2 us (24%)
  waiting for transfers between devices  32.9 us (9%)
  other arithmetic  12.4 us (4%)
  matrix products  10.8 us (3%)
  starting transfers between devices  9.59 us (3%)
    unnamed x36, local copies, waits for them, and re-layouts  57.9 us
    all_gather x4, blocking collectives, all_blocks(): tiles = lax.all_gather(tiles, axes[k], axis=0, tiled=True)  49.6 us
    scatter x2, local copies, waits for them, and re-layouts, shards(): next_spreading_rate = jnp.zeros((layer_heights_count, fill_col), jnp.bflo...  49.2 us
    gather x3, local copies, waits for them, and re-layouts, shards(): message = jnp.take(right_side, column, axis=1, mode='fill', fill_value=0)  44.4 us
    unnamed x2, blocking collectives  34.6 us
    all_to_all x1, waiting for transfers between devices, send_home(): lax.all_to_all(message, GRP_WAVE, split_axis=1, concat_axis=1, tiled=True)  32.9 us
    all_to_all x3, local copies, waits for them, and re-layouts, send_home(): lax.all_to_all(message, GRP_WAVE, split_axis=1, concat_axis=1, tiled=True)  16.8 us
  transfers between devices with their start and end apart: 2, of which 1 were waited for; matrix products, arithmetic and copies ran while one was open for 1% of the time, Pallas kernels for 0%

commit v1 on v0

--- a/solution.py
+++ b/solution.py
@@ -17,7 +17,9 @@
 def all_blocks(shard, axes, turns):
     tiles = shard[None]
     for k in turns:
-        tiles = lax.all_gather(tiles, axes[k], axis=0, tiled=True)
+        tiles = jnp.concatenate(
+            lax.all_to_all(jnp.stack([tiles] * lax.axis_size(axes[k])), axes[k], 0, 0), axis=0
+        )
     held = [lax.axis_size(axes[k]) for k in reversed(turns)]
     tiles = tiles.reshape(*held, *shard.shape)
     turned = sorted(range(len(turns)), key=lambda place: turns[len(turns) - 1 - place])

time: 348 us -> 336 us (0.966)
  blocking collectives: 84.2 us -> 11.1 us
  waiting for transfers between devices: 32.9 us -> 71.6 us
  starting transfers between devices: 9.59 us -> 32.9 us
    all_gather x4 -> x0, blocking collectives: 49.6 us -> none  [all_blocks(): tiles = lax.all_gather(tiles, axes[k], axis=0, tiled=True)]
    unnamed x2 -> x0, blocking collectives: 34.6 us -> none
    all_to_all x1, waiting for transfers between devices: 0.01 us -> 30.1 us  [send_out(): lax.all_to_all(message, GRP_WAVE, split_axis=1, concat_axis=1, tiled=True)]
    all_to_all x0 -> x4, starting transfers between devices: none -> 21.6 us  [all_blocks(): lax.all_to_all(jnp.stack([tiles] * lax.axis_size(axes[k])), axes[k], 0, 0)]
    all_to_all x0 -> x2, blocking collectives: none -> 11.1 us  [all_blocks(): lax.all_to_all(jnp.stack([tiles] * lax.axis_size(axes[k])), axes[k], 0, 0)]
    all_to_all x0 -> x4, waiting for transfers between devices: none -> 8.47 us  [all_blocks(): lax.all_to_all(jnp.stack([tiles] * lax.axis_size(axes[k])), axes[k], 0, 0)]
    unnamed x36 -> x27, local copies, waits for them, and re-layouts: 57.9 us -> 54.7 us
  transfers between devices with their start and end apart: 2 -> 6, of which waited for: 1 -> 4; matrix products, arithmetic and copies ran while one was open for 1% -> 26% of each run, Pallas kernels for 0% -> 0%
where the time goes in v1:
time: 336 us; the launch traced here: 330 us
  local copies, waits for them, and re-layouts  192 us (57%)
  waiting for transfers between devices  71.6 us (21%)
  starting transfers between devices  32.9 us (10%)
  other arithmetic  11.1 us (3%)
  blocking collectives  11.1 us (3%)
  matrix products  10.9 us (3%)
    unnamed x27, local copies, waits for them, and re-layouts  54.7 us
    scatter x2, local copies, waits for them, and re-layouts, shards(): next_spreading_rate = jnp.zeros((layer_heights_count, fill_col), jnp.bflo...  49.2 us
    gather x3, local copies, waits for them, and re-layouts, shards(): message = jnp.take(right_side, column, axis=1, mode='fill', fill_value=0)  44.4 us
    all_to_all x1, waiting for transfers between devices, send_home(): lax.all_to_all(message, GRP_WAVE, split_axis=1, concat_axis=1, tiled=True)  33 us
    all_to_all x1, waiting for transfers between devices, send_out(): lax.all_to_all(message, GRP_WAVE, split_axis=1, concat_axis=1, tiled=True)  30.1 us
    all_to_all x4, starting transfers between devices, all_blocks(): lax.all_to_all(jnp.stack([tiles] * lax.axis_size(axes[k])), axes[k], 0, 0)  21.6 us
    all_to_all x3, local copies, waits for them, and re-layouts, send_home(): lax.all_to_all(message, GRP_WAVE, split_axis=1, concat_axis=1, tiled=True)  16.8 us
    all_to_all x2, blocking collectives, all_blocks(): lax.all_to_all(jnp.stack([tiles] * lax.axis_size(axes[k])), axes[k], 0, 0)  11.1 us
  transfers between devices with their start and end apart: 6, of which 4 were waited for; matrix products, arithmetic and copies ran while one was open for 26% of the time, Pallas kernels for 0%

profile of v1, /device:TPU:1, one launch (start us, length us, event | category | flops | bytes accessed | tf_op | source)
XLA Modules:
  0.0 330.4 jit_solution(13178379724418907945)
XLA Ops:
  0.0 1.3 stack.20
  1.3 5.8 %all-to-all-start.2 = ((s32[4,1,5]{2,1,0:T(1,128)}), s32[4,1,5]{2,1,0:T(1,128)S(1)}, u32[]{:S(2)}, u32[]{:S(2)}) async-start(s32[4,1,5]{2,1,0:T(1,128)} %stack.20), calls=%async_computation.2 | async-start | bytes 4096 | tf_op jit(solution)/shard_map/all_to_all | solution.py:21
  7.1 0.7 broadcast_subtract_fusion.2
  7.8 0.7 add_select_fusion
  8.6 1.0 convert_reduce_fusion
  9.6 0.7 convert_element_type.37
  10.3 4.0 %fusion.4 = bf16[137,7690]{1,0:T(8,128)(2,1)S(1)} fusion(bf16[137,137]{1,0:T(8,128)(2,1)S(1)} %copy-done, f32[7690]{0:T(1024)S(1)} %convert_reduce_fusion, f32[137]{0:T(256)S(1)} %convert_element_type.37, f32[7690]{0:T(1024)S(1)} %fusion.11, bf16[275,7690]{1,0:T(8,128)(2,1)} %param.8), kind=kOutput, calls=%fused_computation.8 | convolution fusion | flops 294988448 | bytes 6704074 | tf_op jit(solution)/shard_map/dot_general | solution.py:113
  14.3 0.6 stack.21
  14.9 4.0 %all-to-all-start.3 = ((s32[4,4,5]{2,1,0:T(4,128)}), s32[4,4,5]{2,1,0:T(4,128)S(1)}, u32[]{:S(2)}, u32[]{:S(2)}) async-start(s32[4,4,5]{2,1,0:T(4,128)} %stack.21), calls=%async_computation.3 | async-start | bytes 16384 | tf_op jit(solution)/shard_map/all_to_all | solution.py:21
  18.9 4.2 %all-to-all-done.3 = s32[4,4,5]{2,1,0:T(4,128)S(1)} async-done(((s32[4,4,5]{2,1,0:T(4,128)}), s32[4,4,5]{2,1,0:T(4,128)S(1)}, u32[]{:S(2)}, u32[]{:S(2)}) %all-to-all-start.3) | async-done | bytes 352 | tf_op jit(solution)/shard_map/all_to_all | solution.py:21
  23.1 0.6 stack.18
  23.7 8.5 %all-to-all-start = ((s32[64,1,3]{2,1,0:T(1,128)}), s32[64,1,3]{2,1,0:T(1,128)S(1)}, u32[]{:S(2)}, u32[]{:S(2)}) async-start(s32[64,1,3]{2,1,0:T(1,128)} %stack.18), calls=%async_computation | async-start | bytes 65536 | tf_op jit(solution)/shard_map/all_to_all | solution.py:21
  32.3 0.1 broadcast_in_dim.117
  32.4 3.7 %copy.111 = bf16[137,7690]{0,1:T(8,128)(2,1)} copy(bf16[137,7690]{1,0:T(8,128)(2,1)S(1)} %fusion.4) | data formatting | bytes 4214120 | tf_op jit(solution)/shard_map/convert_element_type | solution.py:120
  36.2 4.3 %all-to-all-done = s32[64,1,3]{2,1,0:T(1,128)S(1)} async-done(((s32[64,1,3]{2,1,0:T(1,128)}), s32[64,1,3]{2,1,0:T(1,128)S(1)}, u32[]{:S(2)}, u32[]{:S(2)}) %all-to-all-start) | async-done | bytes 800 | tf_op jit(solution)/shard_map/all_to_all | solution.py:21
  40.6 0.1 reshape.257
  40.7 7.4 %all_to_all.45 = s32[2,1,192]{2,1,0:T(1,128)S(1)} all-to-all(s32[2,1,192]{2,1,0:T(1,128)S(1)} %reshape.257), channel_id=1, replica_groups=mesh['grp'=4,'wave_0'=4,'wave_1'=4,'wave_2'=2] {'wave_2'}, dimensions={0} | all-to-all | bytes 3072 | tf_op jit(solution)/shard_map/all_to_all | solution.py:21
  48.2 0.6 stack.22
  48.8 3.2 all-to-all-start.4
  52.0 0.6 broadcast.304
  52.6 0.6 reduce.8
  53.2 0.1 reshape.258
  53.3 0.1 copy.101
  53.4 0.1 le.77
  53.6 0.1 fusion.15
  53.7 0.1 compare_reduce_fusion
  54.0 0.2 copy.103
  54.2 0.2 reshape.228
  54.4 0.1 fusion.9
  54.6 22.6 %gather_fusion = bf16[8448,137]{1,0:T(8,128)(2,1)} fusion(bf16[137,7690]{0,1:T(8,128)(2,1)} %copy.111, s32[9216]{0:T(1024)S(1)} %pad_clamp_fusion), kind=kCustom, calls=%fused_computation | custom fusion | bytes 4663296 | tf_op jit(solution)/shard_map/jit(_take)/gather | solution.py:123
  77.2 5.0 %copy.112 = bf16[137,8448]{1,0:T(8,128)(2,1)S(1)} copy(bf16[137,8448]{0,1:T(8,128)(2,1)} %bitcast.71) | data formatting | bytes 4629504 | tf_op jit(solution)/shard_map/jit(_take)/gather | solution.py:123
  82.2 16.7 %gather.7 = bf16[137,128,66]{2,1,0:T(8,128)(2,1)} reshape(bf16[137,8448]{1,0:T(8,128)(2,1)S(1)} %copy.112) | data formatting | bytes 4629504 | tf_op jit(solution)/shard_map/jit(_take)/gather | solution.py:123
  99.0 0.1 copy.110
  99.1 2.6 broadcast_select_fusion
  101.7 5.0 %copy.133 = bf16[137,128,66]{2,0,1:T(8,128)(2,1)} copy(bf16[137,128,66]{2,1,0:T(8,128)(2,1)S(1)} %broadcast_select_fusion) | data formatting | bytes 4629504 | tf_op jit(solution)/shard_map/jit(_take)/select_n | solution.py:123
  106.7 17.0 %reshape.259 = bf16[128,2,4521]{2,1,0:T(2,128)(2,1)} reshape(bf16[128,137,66]{2,1,0:T(8,128)(2,1)} %bitcast.67) | data formatting | bytes 4629504
  123.9 3.7 %all_to_all.46 = s32[2,1,320]{2,1,0:T(1,128)S(1)} all-to-all(s32[2,1,320]{2,1,0:T(1,128)S(1)} %reshape.261), channel_id=1, replica_groups=mesh['grp'=4,'wave_0'=4,'wave_1'=4,'wave_2'=2] {'wave_2'}, dimensions={0} | all-to-all | bytes 5120 | tf_op jit(solution)/shard_map/all_to_all | solution.py:21
  127.6 6.2 %all-to-all-start.6 = ((bf16[128,2,4521]{2,1,0:T(2,128)(2,1)}), bf16[128,2,4521]{2,1,0:T(2,128)(2,1)S(1)}, u32[]{:S(2)}, u32[]{:S(2)}) async-start(bf16[128,2,4521]{2,1,0:T(2,128)(2,1)} %reshape.259), calls=%async_computation.6 | async-start | bytes 4718592 | tf_op jit(solution)/shard_map/all_to_all | solution.py:34
  133.8 1.4 fusion.16
  135.1 0.6 reduce.9
  135.9 0.1 reshape_reshape.3
  136.0 0.3 copy.107
  136.5 30.1 %all-to-all-done.6 = bf16[128,2,4521]{2,1,0:T(2,128)(2,1)S(1)} async-done(((bf16[128,2,4521]{2,1,0:T(2,128)(2,1)}), bf16[128,2,4521]{2,1,0:T(2,128)(2,1)S(1)}, u32[]{:S(2)}, u32[]{:S(2)}) %all-to-all-start.6) | async-done | bytes 2314784 | tf_op jit(solution)/shard_map/all_to_all | solution.py:34
  166.7 10.2 %reshape.260 = bf16[128,137,66]{2,1,0:T(8,128)(2,1)} reshape(bf16[128,2,4521]{2,1,0:T(2,128)(2,1)S(1)} %all-to-all-done.6) | data formatting | bytes 4629504
  176.9 6.0 %copy.114 = bf16[137,128,66]{1,0,2:T(8,128)(2,1)S(1)} copy(bf16[137,128,66]{2,0,1:T(8,128)(2,1)} %bitcast.68) | data formatting | bytes 4629504 | tf_op jit(solution)/shard_map/all_to_all | solution.py:34
  182.9 0.8 convolution_bitcast_fusion.1
  183.7 0.1 slice.46
  183.8 0.1 copy-done.4
  183.9 0.4 fusion.5
  184.4 0.2 pad_maximum_fusion
  184.6 4.9 %copy.117 = bf16[137,128,66]{2,0,1:T(8,128)(2,1)} copy(bf16[137,128,66]{1,0,2:T(8,128)(2,1)S(1)} %bitcast.75) | data formatting | bytes 4629504 | tf_op jit(solution)/shard_map/convert_element_type | solution.py:52
  189.5 16.8 %reshape.263 = bf16[128,2,4521]{2,1,0:T(2,128)(2,1)} reshape(bf16[128,137,66]{2,1,0:T(8,128)(2,1)} %bitcast.69) | data formatting | bytes 4629504
  206.4 5.2 %all-to-all-start.7 = ((bf16[128,2,4521]{2,1,0:T(2,128)(2,1)}), bf16[128,2,4521]{2,1,0:T(2,128)(2,1)S(1)}, u32[]{:S(2)}, u32[]{:S(2)}) async-start(bf16[128,2,4521]{2,1,0:T(2,128)(2,1)} %reshape.263), calls=%async_computation.7 | async-start | bytes 4718592 | tf_op jit(solution)/shard_map/all_to_all | solution.py:38
  211.7 0.1 broadcast_in_dim.113
  211.8 33.0 %all-to-all-done.7 = bf16[128,2,4521]{2,1,0:T(2,128)(2,1)S(1)} async-done(((bf16[128,2,4521]{2,1,0:T(2,128)(2,1)}), bf16[128,2,4521]{2,1,0:T(2,128)(2,1)S(1)}, u32[]{:S(2)}, u32[]{:S(2)}) %all-to-all-start.7) | async-done | bytes 2314784 | tf_op jit(solution)/shard_map/all_to_all | solution.py:38
  244.8 10.2 %reshape.264 = bf16[128,137,66]{2,1,0:T(8,128)(2,1)} reshape(bf16[128,2,4521]{2,1,0:T(2,128)(2,1)S(1)} %all-to-all-done.7) | data formatting | bytes 4629504
  255.0 5.6 %copy.118 = bf16[137,128,66]{2,1,0:T(8,128)(2,1)} copy(bf16[137,128,66]{2,0,1:T(8,128)(2,1)} %bitcast.70) | data formatting | bytes 4629504 | tf_op jit(solution)/shard_map/all_to_all | solution.py:38
  260.7 7.4 %reshape.241 = bf16[137,8448]{1,0:T(8,128)(2,1)S(1)} reshape(bf16[137,128,66]{2,1,0:T(8,128)(2,1)} %copy.118) | data formatting | bytes 4629504 | tf_op jit(solution)/shard_map/all_to_all | solution.py:38
  268.1 3.8 %copy.119 = bf16[8448,137]{1,0:T(8,128)(2,1)} copy(bf16[8448,137]{0,1:T(8,128)(2,1)S(1)} %bitcast.74) | data formatting | bytes 4629504 | tf_op jit(solution)/shard_map/all_to_all | solution.py:38
  271.9 44.6 %scatter_custom_fusion = bf16[137,7690]{0,1:T(8,128)(2,1)} fusion(s32[8448]{0:T(1024)S(1)} %fusion.9, bf16[8448,137]{1,0:T(8,128)(2,1)} %copy.119, bf16[]{:T(256)} %constant.21.clone.1), kind=kCustom, calls=%fused_computation.17 | custom fusion | bytes 2107572 | tf_op jit(solution)/shard_map/scatter | solution.py:132
  316.5 4.6 %copy.120 = bf16[137,7690]{1,0:T(8,128)(2,1)S(1)} copy(bf16[137,7690]{0,1:T(8,128)(2,1)} %scatter_custom_fusion) | data formatting | bytes 4214120 | tf_op jit(solution)/shard_map/scatter | solution.py:132
  321.1 4.5 %fusion.3 = bf16[137,7690]{1,0:T(8,128)(2,1)S(1)} fusion(bf16[137,7690]{0,1:T(8,128)(2,1)} %scatter_custom_fusion, bf16[137,137]{1,0:T(8,128)(2,1)S(1)} %copy-done.7, bf16[275,7690]{1,0:T(8,128)(2,1)} %param.8), kind=kOutput, calls=%fused_computation.7 | convolution fusion | flops 291827840 | bytes 6358718 | tf_op jit(solution)/shard_map/dot_general | solution.py:136
  325.6 1.1 convolution_reduce_fusion
  326.8 3.3 %maximum_select_fusion = bf16[275,7690]{1,0:T(8,128)(2,1)} fusion(bf16[1,7690]{1,0:T(2,128)(2,1)S(1)} %broadcast_in_dim.131, bf16[137,7690]{1,0:T(8,128)(2,1)S(1)} %fusion.3, bf16[137,7690]{1,0:T(8,128)(2,1)S(1)} %copy.120, pred[7690]{0:T(1024)(128)(4,1)S(1)} %broadcast_in_dim.113), kind=kLoop, calls=%fused_computation.10 | loop fusion | flops 14803250 | bytes 8466690 | tf_op jit(solution)/shard_map/jit(_where)/select_n | solution.py:146
  (58 shorter events, 1.3 us)
Async XLA Ops:
  0.0 10.3 %copy-start = (bf16[137,137]{1,0:T(8,128)(2,1)S(1)}, bf16[137,137]{1,0:T(8,128)(2,1)}, u32[]{:S(2)}) copy-start(bf16[137,137]{1,0:T(8,128)(2,1)} %param.12) | copy-start | bytes 112618
  1.3 13.0 %all-to-all-start.2 = ((s32[4,1,5]{2,1,0:T(1,128)}), s32[4,1,5]{2,1,0:T(1,128)S(1)}, u32[]{:S(2)}, u32[]{:S(2)}) async-start(s32[4,1,5]{2,1,0:T(1,128)} %stack.20), calls=%async_computation.2 | async-start | bytes 4096 | tf_op jit(solution)/shard_map/all_to_all | solution.py:21
  10.3 8.6 %copy-start.5 = (s32[5]{0:T(128)S(1)}, s32[5]{0:T(128)}, u32[]{:S(2)}) copy-start(s32[5]{0:T(128)} %param.9) | copy-start | bytes 64
  10.3 12.8 %copy-start.6 = (s32[3]{0:T(128)S(1)}, s32[3]{0:T(128)}, u32[]{:S(2)}) copy-start(s32[3]{0:T(128)} %param.10) | copy-start | bytes 40
  14.9 8.2 %all-to-all-start.3 = ((s32[4,4,5]{2,1,0:T(4,128)}), s32[4,4,5]{2,1,0:T(4,128)S(1)}, u32[]{:S(2)}, u32[]{:S(2)}) async-start(s32[4,4,5]{2,1,0:T(4,128)} %stack.21), calls=%async_computation.3 | async-start | bytes 16384 | tf_op jit(solution)/shard_map/all_to_all | solution.py:21
  23.7 16.9 %all-to-all-start = ((s32[64,1,3]{2,1,0:T(1,128)}), s32[64,1,3]{2,1,0:T(1,128)S(1)}, u32[]{:S(2)}, u32[]{:S(2)}) async-start(s32[64,1,3]{2,1,0:T(1,128)} %stack.18), calls=%async_computation | async-start | bytes 65536 | tf_op jit(solution)/shard_map/all_to_all | solution.py:21
  48.8 75.0 %all-to-all-start.4 = ((s32[4,16,5]{1,2,0:T(8,128)}), s32[4,16,5]{1,2,0:T(8,128)S(1)}, u32[]{:S(2)}, u32[]{:S(2)}) async-start(s32[4,16,5]{1,2,0:T(8,128)} %stack.22), calls=%async_computation.4 | async-start | bytes 32768 | tf_op jit(solution)/shard_map/all_to_all | solution.py:21
  123.7 10.0 %copy-start.3 = (bf16[3,2,137,137]{3,1,2,0:T(2,128)(2,1)S(1)}, bf16[3,2,137,137]{3,1,2,0:T(2,128)(2,1)}, u32[]{:S(2)}) copy-start(bf16[3,2,137,137]{3,1,2,0:T(2,128)(2,1)} %param.11) | copy-start | bytes 675688
  127.6 39.1 %all-to-all-start.6 = ((bf16[128,2,4521]{2,1,0:T(2,128)(2,1)}), bf16[128,2,4521]{2,1,0:T(2,128)(2,1)S(1)}, u32[]{:S(2)}, u32[]{:S(2)}) async-start(bf16[128,2,4521]{2,1,0:T(2,128)(2,1)} %reshape.259), calls=%async_computation.6 | async-start | bytes 4718592 | tf_op jit(solution)/shard_map/all_to_all | solution.py:34
  182.9 1.0 copy-start.4
  206.3 5.2 %copy-start.8 = (bf16[137]{0:T(256)(128)(2,1)S(1)}, bf16[137]{0:T(256)(128)(2,1)}, u32[]{:S(2)}) copy-start(bf16[137]{0:T(256)(128)(2,1)} %param.15) | copy-start | bytes 826
  206.4 38.5 %all-to-all-start.7 = ((bf16[128,2,4521]{2,1,0:T(2,128)(2,1)}), bf16[128,2,4521]{2,1,0:T(2,128)(2,1)S(1)}, u32[]{:S(2)}, u32[]{:S(2)}) async-start(bf16[128,2,4521]{2,1,0:T(2,128)(2,1)} %reshape.263), calls=%async_computation.7 | async-start | bytes 4718592 | tf_op jit(solution)/shard_map/all_to_all | solution.py:38
  316.5 4.6 %copy-start.7 = (bf16[137,137]{1,0:T(8,128)(2,1)S(1)}, bf16[137,137]{1,0:T(8,128)(2,1)}, u32[]{:S(2)}) copy-start(bf16[137,137]{1,0:T(8,128)(2,1)} %param.14) | copy-start | bytes 112618
  321.1 4.5 %copy-start.2 = (bf16[137,7690]{0,1:T(8,128)(2,1)S(1)}, bf16[137,7690]{0,1:T(8,128)(2,1)}, u32[]{:S(2)}) copy-start(bf16[137,7690]{0,1:T(8,128)(2,1)} %scatter_custom_fusion) | copy-start | bytes 6321184
  326.8 3.4 %copy-start.1 = (bf16[137,137]{1,0:T(8,128)(2,1)S(1)}, bf16[137,137]{1,0:T(8,128)(2,1)}, u32[]{:S(2)}) copy-start(bf16[137,137]{1,0:T(8,128)(2,1)} %param.12) | copy-start | bytes 112618
